TPU v7x, 32 devices: a whole 2x2x4 slice. The times are simulated.
32 devices in a mesh: ep: 8 (over z, y), dp: 4 (over x, core).
Axes of the slice: x: 2, y: 2, z: 4, core: 2. Of those that a mesh axis runs over, the one named last changes fastest.
Arguments:
- tokens_first: bfloat16 [4096, 2048], P(('ep', 'dp')), may hold values from -6 to 6
- routes_first: int32 [4096, 1], P(('ep', 'dp')), may hold values from 0 to 7; in each aligned block of 128 rows (0 to 127, 128 to 255, ...) at most 32 rows name the same one
- gates_first: bfloat16 [4096, 1], P(('ep', 'dp')), may hold values from 0.099609375 to 0.5
- gate_up_weight: bfloat16 [8, 2048, 768], P('ep'), may hold values from -0.125 to 0.125
- down_weight: bfloat16 [8, 384, 2048], P('ep'), may hold values from -0.3125 to 0.3125
- saved_inputs: bfloat16 [8, 4, 256, 2048], P('ep', 'dp'), may hold values from -6 to 6
- upstream: bfloat16 [4096, 2048], P(('ep', 'dp')), may hold values from -0.3984375 to 0.3984375
- routes_second: int32 [4096, 1], P(('ep', 'dp')), may hold values from 0 to 7; in each aligned block of 128 rows (0 to 127, 128 to 255, ...) at most 32 rows name the same one
- gates_second: bfloat16 [4096, 1], P(('ep', 'dp')), may hold values from 0.099609375 to 0.5
Outputs:
- mixed_first: bfloat16 [4096, 2048], P(('ep', 'dp'))
- gate_grads: float32 [4096, 1], P(('ep', 'dp'))
- gate_up_grad: bfloat16 [8, 2048, 768], P('ep', 'dp')
- down_grad: bfloat16 [8, 384, 2048], P('ep', None, 'dp')
Inputs may be any that keep to these rules, and one draw needn't show every extreme that they name: `routes_first`: each row names 1 different experts; in the rows of one device no expert is named more than 32 times, a bound that some block reaches. `routes_second`: each row names 1 different experts; in the rows of one device no expert is named more than 32 times, a bound that some block reaches.
All inputs are finite; a program needn't handle non-finite values.
Results may differ from a plain program's by a relative error of at most 0.014.
Values may be sent and summed in bfloat16 or wider, within the bound.
A program may use at most 64 MiB of HBM per device.

v0:
```python
import functools

import jax
import jax.numpy as jnp
from jax import lax
from jax.experimental import pallas as pl
from jax.experimental.pallas import tpu as pltpu
from jax.sharding import PartitionSpec as P


def slot_places(routing, experts, capacity):
    expert_ids = jnp.arange(experts, dtype=jnp.int32)
    onehot = (routing[:, :, None] == expert_ids).astype(jnp.int32)
    counts = jnp.sum(onehot, axis=1)
    before = jnp.cumsum(counts, axis=0) - counts
    slots = jnp.sum(onehot * before[:, None, :], axis=2)
    return routing * capacity + slots


def local_plain(
    tokens_first,
    routes_first,
    gates_first,
    gate_up_weight,
    down_weight,
    saved_inputs,
    upstream,
    routes_second,
    gates_second,
):
    experts = lax.axis_size("ep")
    capacity = saved_inputs.shape[2] // experts
    places = experts * capacity
    model_width = tokens_first.shape[1]
    weight_gu = gate_up_weight[0]
    weight_down = down_weight[0]
    hidden_size = weight_down.shape[0]

    def expand(places_of):
        lookup = (places_of[:, :, None] == jnp.arange(places, dtype=jnp.int32)).astype(jnp.bfloat16)
        return (lookup, jnp.sum(lookup, axis=1))

    def dispatch(select, values):
        moved = lax.dot_general(
            select, values, (((0,), (0,)), ((), ())), preferred_element_type=jnp.float32
        )
        return moved.astype(jnp.bfloat16).reshape(experts, capacity, model_width)

    def project(inputs):
        return jnp.dot(inputs, weight_gu, preferred_element_type=jnp.float32)

    first_places = slot_places(routes_first, experts, capacity)
    first_lookup, first_select = expand(first_places)
    send_first = dispatch(first_select, tokens_first)
    second_places = slot_places(routes_second, experts, capacity)
    second_lookup, second_select = expand(second_places)
    send_grad = dispatch(second_select, upstream)
    send_gates = jnp.einsum(
        "tkp,tk->p",
        second_lookup.astype(jnp.float32),
        gates_second.astype(jnp.float32),
        precision=lax.Precision.HIGHEST,
    )
    send_gates = send_gates.astype(jnp.bfloat16).reshape(experts, capacity)
    received = lax.all_to_all(send_first, "ep", split_axis=0, concat_axis=0, tiled=True)
    sources = received.shape[0]
    items = received.shape[1]
    projected = project(received.reshape(sources * items, model_width))
    activated = (jax.nn.silu(projected[:, :hidden_size]) * projected[:, hidden_size:]).astype(
        jnp.bfloat16
    )
    outputs = jnp.dot(activated, weight_down, preferred_element_type=jnp.float32).astype(
        jnp.bfloat16
    )
    returned = lax.all_to_all(
        outputs.reshape(sources, items, model_width), "ep", split_axis=0, concat_axis=0, tiled=True
    )
    arrived_grad, arrived_gates = (
        lax.all_to_all(send_grad, "ep", split_axis=0, concat_axis=0, tiled=True),
        lax.all_to_all(send_gates, "ep", split_axis=0, concat_axis=0, tiled=True),
    )
    picked = returned.reshape(places, model_width)[first_places]
    mixed_first = jnp.sum(
        gates_first.astype(jnp.float32)[:, :, None] * picked.astype(jnp.float32), axis=1
    ).astype(jnp.bfloat16)
    saved_rows = saved_inputs[0, 0]
    projected_b = project(saved_rows)
    gate_part = projected_b[:, :hidden_size]
    up_part = projected_b[:, hidden_size:]
    squash = jax.nn.sigmoid(gate_part)
    swish = jax.nn.silu(gate_part)
    activated_b = (swish * up_part).astype(jnp.bfloat16)
    incoming = arrived_grad.reshape(places, model_width)
    gate_column = arrived_gates.reshape(places, 1).astype(jnp.float32)
    grad_hidden = lax.dot_general(
        incoming, weight_down, (((1,), (1,)), ((), ())), preferred_element_type=jnp.float32
    )
    slot_value = jnp.sum(grad_hidden * activated_b.astype(jnp.float32), axis=1)
    returned_value = lax.all_to_all(
        slot_value.reshape(experts, capacity), "ep", split_axis=0, concat_axis=0, tiled=True
    )
    gate_grads = returned_value.reshape(places)[second_places]
    grad_scaled = gate_column * grad_hidden
    grad_gate = grad_scaled * up_part * squash * (1.0 + gate_part * (1.0 - squash))
    grad_up = grad_scaled * swish
    grad_both = jnp.concatenate([grad_gate, grad_up], axis=1).astype(jnp.bfloat16)
    grad_rows = (gate_column * incoming.astype(jnp.float32)).astype(jnp.bfloat16)
    down_term = lax.dot_general(
        activated_b, grad_rows, (((0,), (0,)), ((), ())), preferred_element_type=jnp.float32
    )
    gate_up_term = lax.dot_general(
        saved_rows, grad_both, (((0,), (0,)), ((), ())), preferred_element_type=jnp.float32
    )
    gate_up_grad, down_grad = (
        lax.psum_scatter(
            gate_up_term[None].astype(jnp.bfloat16), "dp", scatter_dimension=1, tiled=True
        ).astype(jnp.float32),
        lax.psum_scatter(
            down_term[None].astype(jnp.bfloat16), "dp", scatter_dimension=2, tiled=True
        ).astype(jnp.float32),
    )
    return (
        mixed_first,
        gate_grads,
        gate_up_grad.astype(jnp.bfloat16),
        down_grad.astype(jnp.bfloat16),
    )


MESH = pl.DeviceIdType.MESH
F32 = jnp.float32
BF16 = jnp.bfloat16


def flipped(index, offset):
    result, bit = index, 1
    while bit <= offset:
        if offset & bit:
            result = result + bit * (1 - 2 * ((index // bit) % 2))
        bit *= 2
    return result


def kernel(
    n_ep,
    n_dp,
    cap,
    routes_1,
    gates_1,
    routes_2,
    gates_2,
    tokens_hbm,
    upstream_hbm,
    gu_hbm,
    down_hbm,
    saved_hbm,
    mixed_hbm,
    ggrad_ref,
    gu_hbm_out,
    dn_hbm_out,
    tokens,
    upstream,
    gu,
    down,
    saved,
    send_1,
    send_2,
    recv_1,
    recv_2,
    outs,
    rets,
    proj,
    act_b,
    both,
    total,
    val_send,
    val_recv,
    term_gu,
    term_dn,
    pair_gu,
    pair_dn,
    sum_gu,
    sum_dn,
    far_gu,
    far_dn,
    mixed,
    gu_out,
    dn_out,
    in_sem,
    out_sem,
    d2_send,
    d2_recv,
    d1_send,
    d1_recv,
    r1_send,
    r1_recv,
    v_send,
    v_recv,
    p_send,
    p_recv,
    f_send,
    f_recv,
):
    me = lax.axis_index("ep")
    me_dp = lax.axis_index("dp")
    parity, chip = me_dp % 2, me_dp // 2
    half = n_dp // 2
    mate = me_dp + 1 - 2 * parity
    count, width = tokens.shape
    hidden = down.shape[0]
    places = n_ep * cap
    upper = [d for d in range(1, n_ep) if d >= n_ep // 2]
    order = [d for d in range(n_ep // 2 - 1, 0, -1)] + upper

    loads = []
    for k, (source, target) in enumerate(
        ((upstream_hbm, upstream), (tokens_hbm, tokens), (saved_hbm, saved), (gu_hbm, gu), (down_hbm, down))
    ):
        copy = pltpu.make_async_copy(source, target, in_sem.at[k])
        copy.start()
        loads.append(copy)

    barrier = pltpu.get_barrier_semaphore()
    for d in range(1, n_ep):
        pl.semaphore_signal(
            barrier, inc=1, device_id=(flipped(me, d), me_dp), device_id_type=MESH
        )
    pl.semaphore_signal(barrier, inc=1, device_id=(me, mate), device_id_type=MESH)
    for t in range(1, half):
        pl.semaphore_signal(
            barrier,
            inc=1,
            device_id=(me, 2 * ((chip + t) % half) + parity),
            device_id_type=MESH,
        )

    def remote(source, target, sends, recvs, to):
        return pltpu.make_async_remote_copy(
            src_ref=source,
            dst_ref=target,
            send_sem=sends,
            recv_sem=recvs,
            device_id=to,
            device_id_type=MESH,
        )

    def placed(routes_ref):
        routes = routes_ref[...]
        rank = lax.broadcasted_iota(jnp.int32, (max(n_ep, 16), count), 0)
        named = jnp.where(rank == routes, 1.0, 0.0)
        earlier = jnp.where(
            lax.broadcasted_iota(jnp.int32, (count, count), 0)
            < lax.broadcasted_iota(jnp.int32, (count, count), 1),
            1.0,
            0.0,
        ).astype(BF16)
        before = jnp.dot(named.astype(BF16), earlier, preferred_element_type=F32)
        slots = jnp.sum(named * before, axis=0, keepdims=True).astype(jnp.int32)
        offset = jnp.bitwise_xor(routes, me)
        return offset, slots

    def column(row):
        return jnp.broadcast_to(row.astype(F32), (count, count)).T

    offset_2, slot_2 = placed(routes_2)
    offset_1, slot_1 = placed(routes_1)
    place_2 = offset_2 * cap + slot_2
    place_1 = offset_1 * cap + slot_1
    slot_ids = lax.broadcasted_iota(jnp.int32, (places, count), 0)

    gate_row_2 = gates_2[...].astype(F32)
    select_2 = jnp.where(slot_ids == place_2, gate_row_2, 0.0).astype(BF16)
    loads[0].wait()
    middle = n_ep // 2
    move_2, move_1 = {}, {}
    for low, high in ((0, middle), (middle, n_ep)):
        send_2[low:high] = (
            jnp.dot(select_2[low * cap : high * cap], upstream[...], preferred_element_type=F32)
            .astype(BF16)
            .reshape(high - low, cap, width)
        )
        if not low:
            pl.semaphore_wait(barrier, n_ep - 1 + half)
        for d in order:
            if low <= d < high:
                move_2[d] = remote(
                    send_2.at[d],
                    recv_2.at[me],
                    d2_send.at[d],
                    d2_recv.at[d],
                    (flipped(me, d), me_dp),
                )
                move_2[d].start()
    recv_2[me] = send_2[0]

    select_1 = jnp.where(slot_ids == place_1, 1.0, 0.0).astype(BF16)
    loads[1].wait()
    send_1[...] = (
        jnp.dot(select_1, tokens[...], preferred_element_type=F32)
        .astype(BF16)
        .reshape(n_ep, cap, width)
    )
    recv_1[0] = send_1[0]
    for d in order:
        move_1[d] = remote(
            send_1.at[d], recv_1.at[d], d1_send.at[d], d1_recv.at[d], (flipped(me, d), me_dp)
        )
        move_1[d].start()

    loads[2].wait()
    loads[3].wait()
    proj[...] = jnp.dot(saved[...], gu[...], preferred_element_type=F32)
    gate = proj[:, :hidden]
    act_b[...] = (gate * jax.nn.sigmoid(gate) * proj[:, hidden:]).astype(BF16)
    loads[4].wait()

    for d in order:
        move_2[d].wait_recv()
    incoming = recv_2[...].reshape(places, width)
    scaled = lax.dot_general(
        incoming, down[...], (((1,), (1,)), ((), ())), preferred_element_type=F32
    )
    product = scaled * act_b[...].astype(F32)
    lanes = product[:, :128]
    for first in range(128, hidden, 128):
        lanes = lanes + product[:, first : first + 128]
    values = jnp.sum(lanes.T, axis=0, keepdims=True)
    val_send[...] = values
    val_recv[0] = values
    move_v = {}
    for d in order:
        move_v[d] = remote(
            val_send, val_recv.at[d], v_send.at[d], v_recv.at[d], (flipped(me, d), me_dp)
        )
        move_v[d].start()
    gate = proj[:, :hidden]
    squash = jax.nn.sigmoid(gate)
    both[:, :hidden] = (
        scaled * proj[:, hidden:] * squash * (1.0 + gate * (1.0 - squash))
    ).astype(BF16)
    both[:, hidden:] = (scaled * (gate * squash)).astype(BF16)

    rows_gu = width // n_dp
    activated_b = act_b[...]
    for j in range(n_dp):
        term_gu[j] = lax.dot_general(
            saved[:, j * rows_gu : (j + 1) * rows_gu],
            both[...],
            (((0,), (0,)), ((), ())),
            preferred_element_type=F32,
        ).astype(BF16)
        term_dn[j] = lax.dot_general(
            activated_b,
            incoming[:, j * rows_gu : (j + 1) * rows_gu],
            (((0,), (0,)), ((), ())),
            preferred_element_type=F32,
        ).astype(BF16)
    move_p = []
    for k in range(half):
        for kind, (term, pair) in enumerate(((term_gu, pair_gu), (term_dn, pair_dn))):
            copy = remote(
                term.at[2 * k + 1 - parity],
                pair.at[k],
                p_send.at[kind, k],
                p_recv.at[kind, k],
                (me, mate),
            )
            copy.start()
            move_p.append(copy)
    for copy in move_p:
        copy.wait_recv()
    move_f = []
    for t in range(1, half):
        k = (chip + t) % half
        for kind, (term, pair, joint, far) in enumerate(
            ((term_gu, pair_gu, sum_gu, far_gu), (term_dn, pair_dn, sum_dn, far_dn))
        ):
            joint[t - 1] = (
                term[2 * k + parity].astype(F32) + pair[k].astype(F32)
            ).astype(BF16)
            copy = remote(
                joint.at[t - 1],
                far.at[t - 1],
                f_send.at[kind, t - 1],
                f_recv.at[kind, t - 1],
                (me, 2 * k + parity),
            )
            copy.start()
            move_f.append(copy)

    groups = list(range(n_ep // 4 - 1, -1, -1)) + list(range(n_ep // 4, n_ep // 2))
    move_r = {}
    for g in groups:
        for d in (2 * g, 2 * g + 1):
            if d:
                move_1[d].wait_recv()
        rows = recv_1[2 * g : 2 * g + 2].reshape(2 * cap, width)
        projected = jnp.dot(rows, gu[...], preferred_element_type=F32)
        first_gate = projected[:, :hidden]
        activated = (first_gate * jax.nn.sigmoid(first_gate) * projected[:, hidden:]).astype(BF16)
        outs[2 * g : 2 * g + 2] = (
            jnp.dot(activated, down[...], preferred_element_type=F32)
            .astype(BF16)
            .reshape(2, cap, width)
        )
        for d in (2 * g, 2 * g + 1):
            if d:
                move_r[d] = remote(
                    outs.at[d], rets.at[d], r1_send.at[d], r1_recv.at[d], (flipped(me, d), me_dp)
                )
                move_r[d].start()
            else:
                rets[0] = outs[0]

    for d in order:
        move_v[d].wait_recv()
    offset_col = column(offset_2)
    wanted = column(slot_2 + me * cap)
    lane_ids = lax.broadcasted_iota(jnp.int32, (count, 128), 1).astype(F32)
    picked = jnp.zeros((count, 128), F32)
    for part in range(places // 128):
        for d in range(n_ep):
            hit = (offset_col[:, :128] == float(d)) & (wanted[:, :128] == lane_ids + 128.0 * part)
            picked = picked + jnp.where(hit, val_recv[d, :, part * 128 : (part + 1) * 128], 0.0)
    ggrad_ref[...] = jnp.sum(picked.T, axis=0, keepdims=True) / gate_row_2

    for copy in move_f:
        copy.wait_recv()
    stores = []
    for number, (term, pair, far, out, target) in enumerate(
        (
            (term_gu, pair_gu, far_gu, gu_out, gu_hbm_out),
            (term_dn, pair_dn, far_dn, dn_out, dn_hbm_out),
        )
    ):
        result = term[me_dp].astype(F32) + pair[chip].astype(F32)
        for t in range(1, half):
            result = result + far[t - 1].astype(F32)
        out[...] = result.astype(BF16)
        copy = pltpu.make_async_copy(out, target, out_sem.at[number])
        copy.start()
        stores.append(copy)

    place_col = column(place_1)
    gate_col = column(gates_1[...])
    group_ids = lax.broadcasted_iota(jnp.int32, (count, 2 * cap), 1).astype(F32)
    last = n_ep // 2 - 1
    for g in range(n_ep // 2):
        for d in (2 * g, 2 * g + 1):
            if d:
                move_r[d].wait_recv()
        lookup = jnp.where(
            place_col[:, : 2 * cap] == group_ids + float(2 * cap * g), gate_col[:, : 2 * cap], 0.0
        ).astype(BF16)
        step = width // 2 if g == last else width
        for first in range(0, width, step):
            columns = slice(first, first + step)
            part = jnp.dot(
                lookup,
                rets[2 * g : 2 * g + 2, :, columns].reshape(2 * cap, step),
                preferred_element_type=F32,
            )
            if g == 0:
                total[:, columns] = part
            elif g < last:
                total[:, columns] += part
            else:
                mixed[:, columns] = (total[:, columns] + part).astype(BF16)
                copy = pltpu.make_async_copy(
                    mixed.at[:, columns], mixed_hbm.at[:, columns], out_sem.at[2 + first // step]
                )
                copy.start()
                stores.append(copy)

    for d in order:
        move_2[d].wait_send()
        move_1[d].wait_send()
        move_r[d].wait_send()
        move_v[d].wait_send()
    for copy in move_p + move_f:
        copy.wait_send()
    for copy in stores:
        copy.wait()


def hand_over(*refs):
    sources, targets, held, in_sem, out_sem = refs[:4], refs[4:8], refs[8:12], refs[12], refs[13]
    loads = [pltpu.make_async_copy(sources[k], held[k], in_sem.at[k]) for k in range(4)]
    stores = [pltpu.make_async_copy(held[k], targets[k], out_sem.at[k]) for k in range(4)]
    for copy in loads:
        copy.start()
    for load, store in zip(loads, stores):
        load.wait()
        store.start()
    for copy in stores:
        copy.wait()


def local(
    tokens_first,
    routes_first,
    gates_first,
    gate_up_weight,
    down_weight,
    saved_inputs,
    upstream,
    routes_second,
    gates_second,
):
    n_ep, n_dp = lax.axis_size("ep"), lax.axis_size("dp")
    cap = saved_inputs.shape[2] // n_ep
    count, top = routes_first.shape
    width = tokens_first.shape[1]
    hidden = down_weight.shape[1]
    places = n_ep * cap
    fits = (
        top == 1
        and cap % 16 == 0
        and 2 * cap <= 128
        and count == 128
        and places % 128 == 0
        and hidden % 128 == 0
        and n_ep >= 4
        and n_ep & (n_ep - 1) == 0
        and n_dp >= 4
        and n_dp % 2 == 0
        and (width // n_dp) % 128 == 0
    )
    if not fits:
        return local_plain(
            tokens_first,
            routes_first,
            gates_first,
            gate_up_weight,
            down_weight,
            saved_inputs,
            upstream,
            routes_second,
            gates_second,
        )
    half, part = n_dp // 2, width // n_dp
    slots = pltpu.VMEM((n_ep, cap, width), BF16)
    dma = pltpu.SemaphoreType.DMA
    vmem, anywhere = pl.BlockSpec(memory_space=pltpu.VMEM), pl.BlockSpec(memory_space=pl.ANY)
    results = (
        jax.ShapeDtypeStruct((count, width), BF16),
        jax.ShapeDtypeStruct((1, count), F32),
        jax.ShapeDtypeStruct((part, 2 * hidden), BF16),
        jax.ShapeDtypeStruct((hidden, part), BF16),
    )
    reached = pl.pallas_call(
        functools.partial(kernel, n_ep, n_dp, cap),
        out_shape=results,
        in_specs=[vmem] * 4 + [anywhere] * 5,
        out_specs=(anywhere, vmem, anywhere, anywhere),
        scratch_shapes=[
            pltpu.VMEM((count, width), BF16),
            pltpu.VMEM((count, width), BF16),
            pltpu.VMEM((width, 2 * hidden), BF16),
            pltpu.VMEM((hidden, width), BF16),
            pltpu.VMEM((places, width), BF16),
            slots,
            slots,
            slots,
            slots,
            slots,
            slots,
            pltpu.VMEM((places, 2 * hidden), F32),
            pltpu.VMEM((places, hidden), BF16),
            pltpu.VMEM((places, 2 * hidden), BF16),
            pltpu.VMEM((count, width), F32),
            pltpu.VMEM((1, places), F32),
            pltpu.VMEM((n_ep, 1, places), F32),
            pltpu.VMEM((n_dp, part, 2 * hidden), BF16),
            pltpu.VMEM((n_dp, hidden, part), BF16),
            pltpu.VMEM((half, part, 2 * hidden), BF16),
            pltpu.VMEM((half, hidden, part), BF16),
            pltpu.VMEM((half - 1, part, 2 * hidden), BF16),
            pltpu.VMEM((half - 1, hidden, part), BF16),
            pltpu.VMEM((half - 1, part, 2 * hidden), BF16),
            pltpu.VMEM((half - 1, hidden, part), BF16),
            pltpu.VMEM((count, width), BF16),
            pltpu.VMEM((part, 2 * hidden), BF16),
            pltpu.VMEM((hidden, part), BF16),
            dma((5,)),
            dma((4,)),
        ]
        + [dma((n_ep,))] * 8
        + [dma((2, half))] * 2
        + [dma((2, half - 1))] * 2,
        compiler_params=pltpu.CompilerParams(
            collective_id=0, has_side_effects=True, vmem_limit_bytes=60 * 1024 * 1024
        ),
    )(
        routes_first.reshape(1, count),
        gates_first.reshape(1, count),
        routes_second.reshape(1, count),
        gates_second.reshape(1, count),
        tokens_first,
        upstream,
        gate_up_weight[0],
        down_weight[0],
        saved_inputs[0, 0],
    )
    mixed, gate_grads, gu_grad, dn_grad = pl.pallas_call(
        hand_over,
        out_shape=results,
        in_specs=[anywhere] * 4,
        out_specs=(anywhere,) * 4,
        scratch_shapes=[pltpu.VMEM(r.shape, r.dtype) for r in results] + [dma((4,))] * 2,
        name="hand_over",
    )(*reached)
    return mixed, gate_grads.reshape(count, 1), gu_grad[None], dn_grad[None]


def solution(mesh):
    return jax.shard_map(
        local,
        mesh=mesh,
        in_specs=(
            P(("ep", "dp"), None),
            P(("ep", "dp"), None),
            P(("ep", "dp"), None),
            P("ep", None, None),
            P("ep", None, None),
            P("ep", "dp", None, None),
            P(("ep", "dp"), None),
            P(("ep", "dp"), None),
            P(("ep", "dp"), None),
        ),
        out_specs=(
            P(("ep", "dp"), None),
            P(("ep", "dp"), None),
            P("ep", "dp", None),
            P("ep", None, "dp"),
        ),
        check_vma=False,
    )
```

profile of v0, /device:TPU:8, one launch (start us, length us, event | category | flops | bytes accessed | tf_op | source)
XLA Modules:
  0.0 78.6 jit_solution(18404003541104452933)
XLA Ops:
  0.6 75.6 %shard_map.120 = (bf16[128,2048]{1,0:T(8,128)(2,1)}, f32[1,128]{1,0:T(1,128)}, bf16[512,768]{1,0:T(8,128)(2,1)}, bf16[384,512]{1,0:T(8,128)(2,1)}) custom-call(s32[1,128]{1,0:T(1,128)} %bitcast.13, bf16[1,128]{1,0:T(2,128)(2,1)} %bitcast.14, s32[1,128]{1,0:T(1,128)} %bitcast.15, bf16[1,128]{1,0:T(2,128)(2,1)} %bitcast.16, bf16[128,2048]{1,0:T(8,128)(2,1)} %tokens_hbm.1, ...), custom_call_target="tpu_custom_call" | custom-call | tf_op jit(solution)/shard_map/pallas_call | solution.py:551
  76.2 2.4 %hand_over.1 = (bf16[128,2048]{1,0:T(8,128)(2,1)}, f32[1,128]{1,0:T(1,128)}, bf16[512,768]{1,0:T(8,128)(2,1)}, bf16[384,512]{1,0:T(8,128)(2,1)}) custom-call(bf16[128,2048]{1,0:T(8,128)(2,1)} %get-tuple-element.12.refs_0_, f32[1,128]{1,0:T(1,128)} %get-tuple-element.13.refs_1_, bf16[512,768]{1,0:T(8,128)(2,1)} %get-tuple-element.14.refs_2_, ...), custom_call_target="tpu_custom_call" | custom-call | tf_op jit(solution)/shard_map/hand_over/pallas_call | solution.py:605
where the time goes:
time: 79 us; the launch traced here: 78.6 us
  Pallas kernels  78 us (99%)
    pallas_call x1, Pallas kernels, local(): pl.pallas_call(functools.partial(kernel, n_ep, n_dp, cap), out_shape=resu...  75.6 us
    pallas_call x1, Pallas kernels, local(): pl.pallas_call(hand_over, out_shape=results, in_specs=[anywhere] * 4, out...  2.37 us

commit v1 on v0

--- a/solution.py
+++ b/solution.py
@@ -145,19 +145,24 @@
     n_ep,
     n_dp,
     cap,
-    routes_1,
-    gates_1,
-    routes_2,
-    gates_2,
+    routes_1_hbm,
+    gates_1_hbm,
+    routes_2_hbm,
+    gates_2_hbm,
     tokens_hbm,
     upstream_hbm,
     gu_hbm,
     down_hbm,
     saved_hbm,
-    mixed_hbm,
+    rets,
+    lookup,
     ggrad_ref,
-    gu_hbm_out,
-    dn_hbm_out,
+    gu_out,
+    dn_out,
+    routes_1,
+    gates_1,
+    routes_2,
+    gates_2,
     tokens,
     upstream,
     gu,
@@ -168,11 +173,9 @@
     recv_1,
     recv_2,
     outs,
-    rets,
     proj,
     act_b,
     both,
-    total,
     val_send,
     val_recv,
     term_gu,
@@ -183,11 +186,7 @@
     sum_dn,
     far_gu,
     far_dn,
-    mixed,
-    gu_out,
-    dn_out,
     in_sem,
-    out_sem,
     d2_send,
     d2_recv,
     d1_send,
@@ -209,19 +208,13 @@
     count, width = tokens.shape
     hidden = down.shape[0]
     places = n_ep * cap
-    upper = [d for d in range(1, n_ep) if d >= n_ep // 2]
-    order = [d for d in range(n_ep // 2 - 1, 0, -1)] + upper
-
-    loads = []
-    for k, (source, target) in enumerate(
-        ((upstream_hbm, upstream), (tokens_hbm, tokens), (saved_hbm, saved), (gu_hbm, gu), (down_hbm, down))
-    ):
-        copy = pltpu.make_async_copy(source, target, in_sem.at[k])
-        copy.start()
-        loads.append(copy)
+    middle = n_ep // 2
+    near = list(range(middle - 1, 0, -1))
+    cross = list(range(middle, n_ep))
+    order = near + cross
 
     barrier = pltpu.get_barrier_semaphore()
-    for d in range(1, n_ep):
+    for d in range(n_ep - 1, 0, -1):
         pl.semaphore_signal(
             barrier, inc=1, device_id=(flipped(me, d), me_dp), device_id_type=MESH
         )
@@ -233,6 +226,25 @@
             device_id=(me, 2 * ((chip + t) % half) + parity),
             device_id_type=MESH,
         )
+
+    loads = [
+        pltpu.make_async_copy(source, target, in_sem.at[k])
+        for k, (source, target) in enumerate(
+            (
+                (routes_2_hbm, routes_2),
+                (gates_2_hbm, gates_2),
+                (upstream_hbm, upstream),
+                (routes_1_hbm, routes_1),
+                (gates_1_hbm, gates_1),
+                (tokens_hbm, tokens),
+                (saved_hbm, saved),
+                (gu_hbm, gu),
+                (down_hbm, down),
+            )
+        )
+    ]
+    for copy in loads[:3]:
+        copy.start()
 
     def remote(source, target, sends, recvs, to):
         return pltpu.make_async_remote_copy(
@@ -262,60 +274,86 @@
     def column(row):
         return jnp.broadcast_to(row.astype(F32), (count, count)).T
 
+    def spread(select, values, target, low, high):
+        target[low:high] = (
+            jnp.dot(select[low * cap : high * cap], values[...], preferred_element_type=F32)
+            .astype(BF16)
+            .reshape(high - low, cap, width)
+        )
+
+    slot_ids = lax.broadcasted_iota(jnp.int32, (places, count), 0)
+
+    def turned(d):
+        if d == 1:
+            return d, flipped(me, 1)
+        base = flipped(me, d - d % 2)
+        swap = parity + (d % 2) * (1 - 2 * parity)
+        return d - d % 2 + swap, base + swap * (1 - 2 * (base % 2))
+
+    def sent_2(d):
+        d, to = turned(d)
+        return remote(send_2.at[d], recv_2.at[me], d2_send.at[d], d2_recv.at[d], (to, me_dp))
+
+    def sent_1(d):
+        d, to = turned(d)
+        return remote(send_1.at[d], recv_1.at[d], d1_send.at[d], d1_recv.at[d], (to, me_dp))
+
+    def sent_r(d):
+        d, to = turned(d)
+        return remote(outs.at[d], rets.at[d], r1_send.at[d], r1_recv.at[d], (to, me_dp))
+
+    move_2 = {d: sent_2(d) for d in order}
+    move_1 = {d: sent_1(d) for d in order}
+    move_r = {d: sent_r(d) for d in order}
+
+    loads[0].wait()
     offset_2, slot_2 = placed(routes_2)
-    offset_1, slot_1 = placed(routes_1)
     place_2 = offset_2 * cap + slot_2
-    place_1 = offset_1 * cap + slot_1
-    slot_ids = lax.broadcasted_iota(jnp.int32, (places, count), 0)
-
+    loads[1].wait()
     gate_row_2 = gates_2[...].astype(F32)
     select_2 = jnp.where(slot_ids == place_2, gate_row_2, 0.0).astype(BF16)
-    loads[0].wait()
-    middle = n_ep // 2
-    move_2, move_1 = {}, {}
-    for low, high in ((0, middle), (middle, n_ep)):
-        send_2[low:high] = (
-            jnp.dot(select_2[low * cap : high * cap], upstream[...], preferred_element_type=F32)
-            .astype(BF16)
-            .reshape(high - low, cap, width)
-        )
-        if not low:
-            pl.semaphore_wait(barrier, n_ep - 1 + half)
-        for d in order:
-            if low <= d < high:
-                move_2[d] = remote(
-                    send_2.at[d],
-                    recv_2.at[me],
-                    d2_send.at[d],
-                    d2_recv.at[d],
-                    (flipped(me, d), me_dp),
-                )
-                move_2[d].start()
+    loads[2].wait()
+    for copy in loads[3:]:
+        copy.start()
+    spread(select_2, upstream, send_2, 0, middle)
+    pl.semaphore_wait(barrier, n_ep - 1 + half)
+    for d in near:
+        move_2[d].start()
+    spread(select_2, upstream, send_2, middle, n_ep)
+    for d in cross:
+        move_2[d].start()
     recv_2[me] = send_2[0]
 
+    loads[3].wait()
+    loads[4].wait()
+    offset_1, slot_1 = placed(routes_1)
+    place_1 = offset_1 * cap + slot_1
     select_1 = jnp.where(slot_ids == place_1, 1.0, 0.0).astype(BF16)
-    loads[1].wait()
-    send_1[...] = (
-        jnp.dot(select_1, tokens[...], preferred_element_type=F32)
-        .astype(BF16)
-        .reshape(n_ep, cap, width)
-    )
+    loads[5].wait()
+    spread(select_1, tokens, send_1, 0, n_ep)
     recv_1[0] = send_1[0]
+
     for d in order:
-        move_1[d] = remote(
-            send_1.at[d], recv_1.at[d], d1_send.at[d], d1_recv.at[d], (flipped(me, d), me_dp)
-        )
         move_1[d].start()
 
-    loads[2].wait()
-    loads[3].wait()
+    place_col = column(place_1)
+    gate_col = column(gates_1[...])
+    lane_col = lax.broadcasted_iota(jnp.int32, (count, 128), 1).astype(F32)
+    for part in range(places // 128):
+        lookup[:, part * 128 : (part + 1) * 128] = jnp.where(
+            place_col[:, :128] == lane_col + float(128 * part), gate_col[:, :128], 0.0
+        ).astype(BF16)
+
+    loads[6].wait()
+    loads[7].wait()
     proj[...] = jnp.dot(saved[...], gu[...], preferred_element_type=F32)
     gate = proj[:, :hidden]
     act_b[...] = (gate * jax.nn.sigmoid(gate) * proj[:, hidden:]).astype(BF16)
-    loads[4].wait()
+    loads[8].wait()
 
     for d in order:
         move_2[d].wait_recv()
+
     incoming = recv_2[...].reshape(places, width)
     scaled = lax.dot_general(
         incoming, down[...], (((1,), (1,)), ((), ())), preferred_element_type=F32
@@ -389,7 +427,6 @@
             move_f.append(copy)
 
     groups = list(range(n_ep // 4 - 1, -1, -1)) + list(range(n_ep // 4, n_ep // 2))
-    move_r = {}
     for g in groups:
         for d in (2 * g, 2 * g + 1):
             if d:
@@ -405,9 +442,6 @@
         )
         for d in (2 * g, 2 * g + 1):
             if d:
-                move_r[d] = remote(
-                    outs.at[d], rets.at[d], r1_send.at[d], r1_recv.at[d], (flipped(me, d), me_dp)
-                )
                 move_r[d].start()
             else:
                 rets[0] = outs[0]
@@ -426,72 +460,51 @@
 
     for copy in move_f:
         copy.wait_recv()
-    stores = []
-    for number, (term, pair, far, out, target) in enumerate(
-        (
-            (term_gu, pair_gu, far_gu, gu_out, gu_hbm_out),
-            (term_dn, pair_dn, far_dn, dn_out, dn_hbm_out),
-        )
+    for term, pair, far, out in (
+        (term_gu, pair_gu, far_gu, gu_out),
+        (term_dn, pair_dn, far_dn, dn_out),
     ):
         result = term[me_dp].astype(F32) + pair[chip].astype(F32)
         for t in range(1, half):
             result = result + far[t - 1].astype(F32)
         out[...] = result.astype(BF16)
-        copy = pltpu.make_async_copy(out, target, out_sem.at[number])
-        copy.start()
-        stores.append(copy)
-
-    place_col = column(place_1)
-    gate_col = column(gates_1[...])
-    group_ids = lax.broadcasted_iota(jnp.int32, (count, 2 * cap), 1).astype(F32)
-    last = n_ep // 2 - 1
-    for g in range(n_ep // 2):
-        for d in (2 * g, 2 * g + 1):
-            if d:
-                move_r[d].wait_recv()
-        lookup = jnp.where(
-            place_col[:, : 2 * cap] == group_ids + float(2 * cap * g), gate_col[:, : 2 * cap], 0.0
-        ).astype(BF16)
-        step = width // 2 if g == last else width
-        for first in range(0, width, step):
-            columns = slice(first, first + step)
-            part = jnp.dot(
-                lookup,
-                rets[2 * g : 2 * g + 2, :, columns].reshape(2 * cap, step),
-                preferred_element_type=F32,
-            )
-            if g == 0:
-                total[:, columns] = part
-            elif g < last:
-                total[:, columns] += part
-            else:
-                mixed[:, columns] = (total[:, columns] + part).astype(BF16)
-                copy = pltpu.make_async_copy(
-                    mixed.at[:, columns], mixed_hbm.at[:, columns], out_sem.at[2 + first // step]
-                )
-                copy.start()
-                stores.append(copy)
 
     for d in order:
         move_2[d].wait_send()
         move_1[d].wait_send()
-        move_r[d].wait_send()
         move_v[d].wait_send()
     for copy in move_p + move_f:
         copy.wait_send()
+    for d in order:
+        move_r[d].wait_recv()
+    for d in order:
+        move_r[d].wait_send()
+
+
+def finish(
+    rets, lookup, ggrad, gu_grad, dn_grad, mixed_hbm, ggrad_hbm, gu_hbm, dn_hbm, mixed, out_sem
+):
+    stores = [
+        pltpu.make_async_copy(source, target, out_sem.at[k])
+        for k, (source, target) in enumerate(
+            ((gu_grad, gu_hbm), (dn_grad, dn_hbm), (ggrad, ggrad_hbm))
+        )
+    ]
     for copy in stores:
-        copy.wait()
-
-
-def hand_over(*refs):
-    sources, targets, held, in_sem, out_sem = refs[:4], refs[4:8], refs[8:12], refs[12], refs[13]
-    loads = [pltpu.make_async_copy(sources[k], held[k], in_sem.at[k]) for k in range(4)]
-    stores = [pltpu.make_async_copy(held[k], targets[k], out_sem.at[k]) for k in range(4)]
-    for copy in loads:
         copy.start()
-    for load, store in zip(loads, stores):
-        load.wait()
-        store.start()
+    width = mixed.shape[1]
+    slots = rets.shape[0] * rets.shape[1]
+    step = width // 4
+    for number in range(4):
+        columns = slice(number * step, (number + 1) * step)
+        mixed[:, columns] = jnp.dot(
+            lookup[...], rets[:, :, columns].reshape(slots, step), preferred_element_type=F32
+        ).astype(BF16)
+        copy = pltpu.make_async_copy(
+            mixed.at[:, columns], mixed_hbm.at[:, columns], out_sem.at[3 + number]
+        )
+        copy.start()
+        stores.append(copy)
     for copy in stores:
         copy.wait()
 
@@ -542,18 +555,22 @@
     slots = pltpu.VMEM((n_ep, cap, width), BF16)
     dma = pltpu.SemaphoreType.DMA
     vmem, anywhere = pl.BlockSpec(memory_space=pltpu.VMEM), pl.BlockSpec(memory_space=pl.ANY)
-    results = (
-        jax.ShapeDtypeStruct((count, width), BF16),
-        jax.ShapeDtypeStruct((1, count), F32),
-        jax.ShapeDtypeStruct((part, 2 * hidden), BF16),
-        jax.ShapeDtypeStruct((hidden, part), BF16),
-    )
     reached = pl.pallas_call(
         functools.partial(kernel, n_ep, n_dp, cap),
-        out_shape=results,
-        in_specs=[vmem] * 4 + [anywhere] * 5,
-        out_specs=(anywhere, vmem, anywhere, anywhere),
+        out_shape=(
+            slots,
+            pltpu.VMEM((count, places), BF16),
+            pltpu.VMEM((1, count), F32),
+            pltpu.VMEM((part, 2 * hidden), BF16),
+            pltpu.VMEM((hidden, part), BF16),
+        ),
+        in_specs=[anywhere] * 9,
+        out_specs=(vmem,) * 5,
         scratch_shapes=[
+            pltpu.VMEM((1, count), jnp.int32),
+            pltpu.VMEM((1, count), BF16),
+            pltpu.VMEM((1, count), jnp.int32),
+            pltpu.VMEM((1, count), BF16),
             pltpu.VMEM((count, width), BF16),
             pltpu.VMEM((count, width), BF16),
             pltpu.VMEM((width, 2 * hidden), BF16),
@@ -564,11 +581,9 @@
             slots,
             slots,
             slots,
-            slots,
             pltpu.VMEM((places, 2 * hidden), F32),
             pltpu.VMEM((places, hidden), BF16),
             pltpu.VMEM((places, 2 * hidden), BF16),
-            pltpu.VMEM((count, width), F32),
             pltpu.VMEM((1, places), F32),
             pltpu.VMEM((n_ep, 1, places), F32),
             pltpu.VMEM((n_dp, part, 2 * hidden), BF16),
@@ -579,37 +594,43 @@
             pltpu.VMEM((half - 1, hidden, part), BF16),
             pltpu.VMEM((half - 1, part, 2 * hidden), BF16),
             pltpu.VMEM((half - 1, hidden, part), BF16),
-            pltpu.VMEM((count, width), BF16),
-            pltpu.VMEM((part, 2 * hidden), BF16),
-            pltpu.VMEM((hidden, part), BF16),
-            dma((5,)),
-            dma((4,)),
+            dma((9,)),
         ]
         + [dma((n_ep,))] * 8
         + [dma((2, half))] * 2
         + [dma((2, half - 1))] * 2,
         compiler_params=pltpu.CompilerParams(
-            collective_id=0, has_side_effects=True, vmem_limit_bytes=60 * 1024 * 1024
+            collective_id=0, has_side_effects=True, vmem_limit_bytes=44 * 1024 * 1024
         ),
     )(
-        routes_first.reshape(1, count),
-        gates_first.reshape(1, count),
-        routes_second.reshape(1, count),
-        gates_second.reshape(1, count),
-        tokens_first,
-        upstream,
-        gate_up_weight[0],
-        down_weight[0],
-        saved_inputs[0, 0],
+        *(
+            pltpu.with_memory_space_constraint(value, pltpu.HBM)
+            for value in (
+                routes_first.reshape(1, count),
+                gates_first.reshape(1, count),
+                routes_second.reshape(1, count),
+                gates_second.reshape(1, count),
+                tokens_first,
+                upstream,
+                gate_up_weight[0],
+                down_weight[0],
+                saved_inputs[0, 0],
+            )
+        )
     )
     mixed, gate_grads, gu_grad, dn_grad = pl.pallas_call(
-        hand_over,
-        out_shape=results,
-        in_specs=[anywhere] * 4,
+        finish,
+        out_shape=(
+            jax.ShapeDtypeStruct((count, width), BF16),
+            jax.ShapeDtypeStruct((1, count), F32),
+            jax.ShapeDtypeStruct((part, 2 * hidden), BF16),
+            jax.ShapeDtypeStruct((hidden, part), BF16),
+        ),
+        in_specs=[vmem] * 5,
         out_specs=(anywhere,) * 4,
-        scratch_shapes=[pltpu.VMEM(r.shape, r.dtype) for r in results] + [dma((4,))] * 2,
-        name="hand_over",
-    )(*reached)
+        scratch_shapes=[pltpu.VMEM((count, width), BF16), dma((7,))],
+        name="finish",
+    )(*(pltpu.with_memory_space_constraint(value, pltpu.VMEM) for value in reached))
     return mixed, gate_grads.reshape(count, 1), gu_grad[None], dn_grad[None]
 
 

time: 79 us -> 75.5 us (0.956)
  Pallas kernels: 78 us -> 74.7 us
    pallas_call x2, Pallas kernels: 78 us -> 74.7 us  [the longest x1 73.4 us: local(): pl.pallas_call(functools.partial(kernel, n_ep, n_dp, cap), out_shape=(slo...]
where the time goes in v1:
time: 75.5 us; the launch traced here: 75.3 us
  Pallas kernels  74.7 us (99%)
    pallas_call x1, Pallas kernels, local(): pl.pallas_call(functools.partial(kernel, n_ep, n_dp, cap), out_shape=(slo...  73.4 us

profile of v1, /device:TPU:8, one launch (start us, length us, event | category | flops | bytes accessed | tf_op | source)
XLA Modules:
  0.0 75.3 jit_solution(14938574372053178881)
XLA Ops:
  0.6 73.4 %shard_map.120 = (bf16[8,32,2048]{2,1,0:T(8,128)(2,1)S(1)}, bf16[128,256]{1,0:T(8,128)(2,1)S(1)}, f32[1,128]{1,0:T(1,128)S(1)}, bf16[512,768]{1,0:T(8,128)(2,1)S(1)}, bf16[384,512]{1,0:T(8,128)(2,1)S(1)}) custom-call(s32[1,128]{1,0:T(1,128)} %bitcast.13, bf16[1,128]{1,0:T(2,128)(2,1)} %bitcast.14, s32[1,128]{1,0:T(1,128)} %bitcast.15, ...), custom_call_target="tpu_custom_call" | custom-call | tf_op jit(solution)/shard_map/pallas_call | solution.py:558
  74.1 1.2 %finish.1 = (bf16[128,2048]{1,0:T(8,128)(2,1)}, f32[1,128]{1,0:T(1,128)}, bf16[512,768]{1,0:T(8,128)(2,1)}, bf16[384,512]{1,0:T(8,128)(2,1)}) custom-call(bf16[8,32,2048]{2,1,0:T(8,128)(2,1)S(1)} %get-tuple-element.13.rets, bf16[128,256]{1,0:T(8,128)(2,1)S(1)} %get-tuple-element.14.lookup, f32[1,128]{1,0:T(1,128)S(1)} %get-tuple-element.15.ggrad, ...), custom_call_target="tpu_custom_call" | custom-call | tf_op jit(solution)/shard_map/finish/pallas_call | solution.py:621

commit v2 on v1

--- a/solution.py
+++ b/solution.py
@@ -213,19 +213,9 @@
     cross = list(range(middle, n_ep))
     order = near + cross
 
-    barrier = pltpu.get_barrier_semaphore()
-    for d in range(n_ep - 1, 0, -1):
-        pl.semaphore_signal(
-            barrier, inc=1, device_id=(flipped(me, d), me_dp), device_id_type=MESH
-        )
-    pl.semaphore_signal(barrier, inc=1, device_id=(me, mate), device_id_type=MESH)
-    for t in range(1, half):
-        pl.semaphore_signal(
-            barrier,
-            inc=1,
-            device_id=(me, 2 * ((chip + t) % half) + parity),
-            device_id_type=MESH,
-        )
+    quarter = me // (n_ep // 4)
+    inner = (quarter == 1) | (quarter == 2)
+    outer = (quarter == 0) | (quarter == 3)
 
     loads = [
         pltpu.make_async_copy(source, target, in_sem.at[k])
@@ -246,6 +236,20 @@
     for copy in loads[:3]:
         copy.start()
 
+    barrier = pltpu.get_barrier_semaphore()
+    for d in range(n_ep - 1, 0, -1):
+        pl.semaphore_signal(
+            barrier, inc=1, device_id=(flipped(me, d), me_dp), device_id_type=MESH
+        )
+    pl.semaphore_signal(barrier, inc=1, device_id=(me, mate), device_id_type=MESH)
+    for t in range(1, half):
+        pl.semaphore_signal(
+            barrier,
+            inc=1,
+            device_id=(me, 2 * ((chip + t) % half) + parity),
+            device_id_type=MESH,
+        )
+
     def remote(source, target, sends, recvs, to):
         return pltpu.make_async_remote_copy(
             src_ref=source,
@@ -290,21 +294,30 @@
         swap = parity + (d % 2) * (1 - 2 * parity)
         return d - d % 2 + swap, base + swap * (1 - 2 * (base % 2))
 
-    def sent_2(d):
-        d, to = turned(d)
-        return remote(send_2.at[d], recv_2.at[me], d2_send.at[d], d2_recv.at[d], (to, me_dp))
-
-    def sent_1(d):
-        d, to = turned(d)
-        return remote(send_1.at[d], recv_1.at[d], d1_send.at[d], d1_recv.at[d], (to, me_dp))
-
-    def sent_r(d):
-        d, to = turned(d)
-        return remote(outs.at[d], rets.at[d], r1_send.at[d], r1_recv.at[d], (to, me_dp))
-
-    move_2 = {d: sent_2(d) for d in order}
-    move_1 = {d: sent_1(d) for d in order}
-    move_r = {d: sent_r(d) for d in order}
+    def start(kind, numbers):
+        source, target, sends, recvs = {
+            1: (send_1, recv_1, d1_send, d1_recv),
+            2: (send_2, recv_2, d2_send, d2_recv),
+            3: (outs, rets, r1_send, r1_recv),
+        }[kind]
+        pieces = 2
+        for pair in dict.fromkeys(d // 2 for d in numbers):
+            for piece in range(pieces):
+                rows = slice(piece * cap // pieces, (piece + 1) * cap // pieces)
+                for number in numbers:
+                    if number // 2 == pair:
+                        d, to = turned(number)
+                        remote(
+                            source.at[d, rows],
+                            target.at[me if kind == 2 else d, rows],
+                            sends,
+                            recvs.at[pair] if kind == 1 else recvs,
+                            (to, me_dp),
+                        ).start()
+
+    def several(source, target, sends, recvs):
+        return remote(source, target, sends, recvs, (me, mate))
+
 
     loads[0].wait()
     offset_2, slot_2 = placed(routes_2)
@@ -315,13 +328,20 @@
     loads[2].wait()
     for copy in loads[3:]:
         copy.start()
+    spread(select_2, upstream, send_2, middle, n_ep)
+    pl.semaphore_wait(barrier, n_ep - 1 + half)
+
+    @pl.when(inner)
+    def _():
+        start(2, cross[middle // 2 :] + cross[: middle // 2])
+
     spread(select_2, upstream, send_2, 0, middle)
-    pl.semaphore_wait(barrier, n_ep - 1 + half)
-    for d in near:
-        move_2[d].start()
-    spread(select_2, upstream, send_2, middle, n_ep)
-    for d in cross:
-        move_2[d].start()
+    start(2, near)
+
+    @pl.when(outer)
+    def _():
+        start(2, cross)
+
     recv_2[me] = send_2[0]
 
     loads[3].wait()
@@ -333,8 +353,12 @@
     spread(select_1, tokens, send_1, 0, n_ep)
     recv_1[0] = send_1[0]
 
-    for d in order:
-        move_1[d].start()
+    start(1, near)
+
+    @pl.when(inner)
+    def _():
+        start(1, cross)
+
 
     place_col = column(place_1)
     gate_col = column(gates_1[...])
@@ -351,8 +375,13 @@
     act_b[...] = (gate * jax.nn.sigmoid(gate) * proj[:, hidden:]).astype(BF16)
     loads[8].wait()
 
-    for d in order:
-        move_2[d].wait_recv()
+    others = slice(1, n_ep)
+    several(send_2.at[others], recv_2.at[others], d2_send, d2_recv).wait_recv()
+
+    @pl.when(outer)
+    def _():
+        start(1, cross)
+
 
     incoming = recv_2[...].reshape(places, width)
     scaled = lax.dot_general(
@@ -368,7 +397,7 @@
     move_v = {}
     for d in order:
         move_v[d] = remote(
-            val_send, val_recv.at[d], v_send.at[d], v_recv.at[d], (flipped(me, d), me_dp)
+            val_send, val_recv.at[d], v_send, v_recv, (flipped(me, d), me_dp)
         )
         move_v[d].start()
     gate = proj[:, :hidden]
@@ -393,21 +422,21 @@
             (((0,), (0,)), ((), ())),
             preferred_element_type=F32,
         ).astype(BF16)
-    move_p = []
     for k in range(half):
         for kind, (term, pair) in enumerate(((term_gu, pair_gu), (term_dn, pair_dn))):
-            copy = remote(
+            remote(
                 term.at[2 * k + 1 - parity],
                 pair.at[k],
-                p_send.at[kind, k],
-                p_recv.at[kind, k],
+                p_send.at[kind],
+                p_recv.at[kind],
                 (me, mate),
-            )
-            copy.start()
-            move_p.append(copy)
-    for copy in move_p:
+            ).start()
+    moved_p = [
+        several(term.at[:half], pair, p_send.at[kind], p_recv.at[kind])
+        for kind, (term, pair) in enumerate(((term_gu, pair_gu), (term_dn, pair_dn)))
+    ]
+    for copy in moved_p:
         copy.wait_recv()
-    move_f = []
     for t in range(1, half):
         k = (chip + t) % half
         for kind, (term, pair, joint, far) in enumerate(
@@ -416,21 +445,22 @@
             joint[t - 1] = (
                 term[2 * k + parity].astype(F32) + pair[k].astype(F32)
             ).astype(BF16)
-            copy = remote(
+            remote(
                 joint.at[t - 1],
                 far.at[t - 1],
-                f_send.at[kind, t - 1],
-                f_recv.at[kind, t - 1],
+                f_send.at[kind],
+                f_recv.at[kind],
                 (me, 2 * k + parity),
-            )
-            copy.start()
-            move_f.append(copy)
+            ).start()
+    moved_f = [
+        several(joint, far, f_send.at[kind], f_recv.at[kind])
+        for kind, (joint, far) in enumerate(((sum_gu, far_gu), (sum_dn, far_dn)))
+    ]
 
     groups = list(range(n_ep // 4 - 1, -1, -1)) + list(range(n_ep // 4, n_ep // 2))
     for g in groups:
-        for d in (2 * g, 2 * g + 1):
-            if d:
-                move_1[d].wait_recv()
+        pair = slice(2 * g if g else 1, 2 * g + 2)
+        several(send_1.at[pair], recv_1.at[pair], d1_send, d1_recv.at[g]).wait_recv()
         rows = recv_1[2 * g : 2 * g + 2].reshape(2 * cap, width)
         projected = jnp.dot(rows, gu[...], preferred_element_type=F32)
         first_gate = projected[:, :hidden]
@@ -440,14 +470,11 @@
             .astype(BF16)
             .reshape(2, cap, width)
         )
-        for d in (2 * g, 2 * g + 1):
-            if d:
-                move_r[d].start()
-            else:
-                rets[0] = outs[0]
-
-    for d in order:
-        move_v[d].wait_recv()
+        start(3, [d for d in (2 * g, 2 * g + 1) if d])
+        if g == 0:
+            rets[0] = outs[0]
+
+    several(val_recv.at[others], val_recv.at[others], v_send, v_recv).wait_recv()
     offset_col = column(offset_2)
     wanted = column(slot_2 + me * cap)
     lane_ids = lax.broadcasted_iota(jnp.int32, (count, 128), 1).astype(F32)
@@ -458,7 +485,7 @@
             picked = picked + jnp.where(hit, val_recv[d, :, part * 128 : (part + 1) * 128], 0.0)
     ggrad_ref[...] = jnp.sum(picked.T, axis=0, keepdims=True) / gate_row_2
 
-    for copy in move_f:
+    for copy in moved_f:
         copy.wait_recv()
     for term, pair, far, out in (
         (term_gu, pair_gu, far_gu, gu_out),
@@ -469,16 +496,14 @@
             result = result + far[t - 1].astype(F32)
         out[...] = result.astype(BF16)
 
-    for d in order:
-        move_2[d].wait_send()
-        move_1[d].wait_send()
-        move_v[d].wait_send()
-    for copy in move_p + move_f:
+    several(send_2.at[others], recv_2.at[others], d2_send, d2_recv).wait_send()
+    several(send_1.at[others], recv_1.at[others], d1_send, d1_recv.at[0]).wait_send()
+    several(val_recv.at[others], val_recv.at[others], v_send, v_recv).wait_send()
+    for copy in moved_p + moved_f:
         copy.wait_send()
-    for d in order:
-        move_r[d].wait_recv()
-    for d in order:
-        move_r[d].wait_send()
+    returned = several(outs.at[others], rets.at[others], r1_send, r1_recv)
+    returned.wait_send()
+    returned.wait_recv()
 
 
 def finish(
@@ -596,9 +621,9 @@
             pltpu.VMEM((half - 1, hidden, part), BF16),
             dma((9,)),
         ]
-        + [dma((n_ep,))] * 8
-        + [dma((2, half))] * 2
-        + [dma((2, half - 1))] * 2,
+        + [dma(()), dma(()), dma(()), dma((n_ep // 2,))]
+        + [dma(())] * 4
+        + [dma((2,))] * 4,
         compiler_params=pltpu.CompilerParams(
             collective_id=0, has_side_effects=True, vmem_limit_bytes=44 * 1024 * 1024
         ),

time: 75.5 us -> 74.6 us (0.988)
  Pallas kernels: 74.7 us -> 73.8 us
    pallas_call x1, Pallas kernels: 73.4 us -> 72.5 us  [local(): pl.pallas_call(functools.partial(kernel, n_ep, n_dp, cap), out_shape=(slo...]
where the time goes in v2:
time: 74.6 us; the launch traced here: 74.4 us
  Pallas kernels  73.8 us (99%)
    pallas_call x1, Pallas kernels, local(): pl.pallas_call(functools.partial(kernel, n_ep, n_dp, cap), out_shape=(slo...  72.5 us

profile of v2, /device:TPU:8, one launch (start us, length us, event | category | flops | bytes accessed | tf_op | source)
XLA Modules:
  0.0 74.4 jit_solution(7253097628327905401)
XLA Ops:
  0.6 72.5 %shard_map.120 = (bf16[8,32,2048]{2,1,0:T(8,128)(2,1)S(1)}, bf16[128,256]{1,0:T(8,128)(2,1)S(1)}, f32[1,128]{1,0:T(1,128)S(1)}, bf16[512,768]{1,0:T(8,128)(2,1)S(1)}, bf16[384,512]{1,0:T(8,128)(2,1)S(1)}) custom-call(s32[1,128]{1,0:T(1,128)} %bitcast.13, bf16[1,128]{1,0:T(2,128)(2,1)} %bitcast.14, s32[1,128]{1,0:T(1,128)} %bitcast.15, ...), custom_call_target="tpu_custom_call" | custom-call | tf_op jit(solution)/shard_map/pallas_call | solution.py:583
  73.2 1.2 %finish.1 = (bf16[128,2048]{1,0:T(8,128)(2,1)}, f32[1,128]{1,0:T(1,128)}, bf16[512,768]{1,0:T(8,128)(2,1)}, bf16[384,512]{1,0:T(8,128)(2,1)}) custom-call(bf16[8,32,2048]{2,1,0:T(8,128)(2,1)S(1)} %get-tuple-element.13.rets, bf16[128,256]{1,0:T(8,128)(2,1)S(1)} %get-tuple-element.14.lookup, f32[1,128]{1,0:T(1,128)S(1)} %get-tuple-element.15.ggrad, ...), custom_call_target="tpu_custom_call" | custom-call | tf_op jit(solution)/shard_map/finish/pallas_call | solution.py:646

commit v3 on v2

--- a/solution.py
+++ b/solution.py
@@ -236,11 +236,17 @@
     for copy in loads[:3]:
         copy.start()
 
+    kin = [d for d in range(n_ep - 1, 0, -1) if d // (n_ep // 4) in (0, 3)]
+    strange = [d for d in range(n_ep - 1, 0, -1) if d not in kin]
     barrier = pltpu.get_barrier_semaphore()
-    for d in range(n_ep - 1, 0, -1):
-        pl.semaphore_signal(
-            barrier, inc=1, device_id=(flipped(me, d), me_dp), device_id_type=MESH
-        )
+
+    def greet(numbers):
+        for d in numbers:
+            pl.semaphore_signal(
+                barrier, inc=1, device_id=(flipped(me, d), me_dp), device_id_type=MESH
+            )
+
+    greet(kin)
     pl.semaphore_signal(barrier, inc=1, device_id=(me, mate), device_id_type=MESH)
     for t in range(1, half):
         pl.semaphore_signal(
@@ -287,11 +293,11 @@
 
     slot_ids = lax.broadcasted_iota(jnp.int32, (places, count), 0)
 
-    def turned(d):
+    def turned(d, side):
         if d == 1:
             return d, flipped(me, 1)
         base = flipped(me, d - d % 2)
-        swap = parity + (d % 2) * (1 - 2 * parity)
+        swap = side + (d % 2) * (1 - 2 * side)
         return d - d % 2 + swap, base + swap * (1 - 2 * (base % 2))
 
     def start(kind, numbers):
@@ -302,18 +308,21 @@
         }[kind]
         pieces = 2
         for pair in dict.fromkeys(d // 2 for d in numbers):
-            for piece in range(pieces):
+            members = [d for d in numbers if d // 2 == pair]
+            last = kind == 3 and pair == n_ep // 2 - 1
+            pairs = [(piece, number) for piece in range(pieces) for number in members]
+            if last:
+                pairs.sort(key=lambda entry: entry[1])
+            for piece, number in pairs:
                 rows = slice(piece * cap // pieces, (piece + 1) * cap // pieces)
-                for number in numbers:
-                    if number // 2 == pair:
-                        d, to = turned(number)
-                        remote(
-                            source.at[d, rows],
-                            target.at[me if kind == 2 else d, rows],
-                            sends,
-                            recvs.at[pair] if kind == 1 else recvs,
-                            (to, me_dp),
-                        ).start()
+                d, to = turned(number, me % 2 if last else parity)
+                remote(
+                    source.at[d, rows],
+                    target.at[me if kind == 2 else d, rows],
+                    sends,
+                    recvs.at[pair] if kind == 1 else recvs,
+                    (to, me_dp),
+                ).start()
 
     def several(source, target, sends, recvs):
         return remote(source, target, sends, recvs, (me, mate))
@@ -329,20 +338,22 @@
     for copy in loads[3:]:
         copy.start()
     spread(select_2, upstream, send_2, middle, n_ep)
-    pl.semaphore_wait(barrier, n_ep - 1 + half)
+    ahead, behind = cross[middle // 2 :], cross[: middle // 2]
 
     @pl.when(inner)
     def _():
-        start(2, cross[middle // 2 :] + cross[: middle // 2])
+        pl.semaphore_wait(barrier, len(kin) + half)
+        greet(strange)
+        start(2, ahead)
 
     spread(select_2, upstream, send_2, 0, middle)
-    start(2, near)
+    recv_2[me] = send_2[0]
 
     @pl.when(outer)
     def _():
-        start(2, cross)
-
-    recv_2[me] = send_2[0]
+        pl.semaphore_wait(barrier, len(kin) + half + len(strange))
+        greet(strange)
+        start(2, order)
 
     loads[3].wait()
     loads[4].wait()
@@ -353,12 +364,15 @@
     spread(select_1, tokens, send_1, 0, n_ep)
     recv_1[0] = send_1[0]
 
-    start(1, near)
-
     @pl.when(inner)
     def _():
-        start(1, cross)
-
+        pl.semaphore_wait(barrier, len(strange))
+        start(2, near + behind)
+        start(1, near + cross)
+
+    @pl.when(outer)
+    def _():
+        start(1, near)
 
     place_col = column(place_1)
     gate_col = column(gates_1[...])

time: 74.6 us -> 73.9 us (level); the launches traced: 74.4 us -> 72.7 us
  Pallas kernels: 73.8 us -> 72.1 us
    pallas_call x1, Pallas kernels: 72.5 us -> 70.8 us  [local(): pl.pallas_call(functools.partial(kernel, n_ep, n_dp, cap), out_shape=(slo...]
where the time goes in v3:
time: 73.9 us; the launch traced here: 72.7 us
  Pallas kernels  72.1 us (98%)
    pallas_call x1, Pallas kernels, local(): pl.pallas_call(functools.partial(kernel, n_ep, n_dp, cap), out_shape=(slo...  70.8 us

profile of v3, /device:TPU:8, one launch (start us, length us, event | category | flops | bytes accessed | tf_op | source)
XLA Modules:
  0.0 72.7 jit_solution(6843704055126012017)
XLA Ops:
  0.6 70.8 %shard_map.120 = (bf16[8,32,2048]{2,1,0:T(8,128)(2,1)S(1)}, bf16[128,256]{1,0:T(8,128)(2,1)S(1)}, f32[1,128]{1,0:T(1,128)S(1)}, bf16[512,768]{1,0:T(8,128)(2,1)S(1)}, bf16[384,512]{1,0:T(8,128)(2,1)S(1)}) custom-call(s32[1,128]{1,0:T(1,128)} %bitcast.13, bf16[1,128]{1,0:T(2,128)(2,1)} %bitcast.14, s32[1,128]{1,0:T(1,128)} %bitcast.15, ...), custom_call_target="tpu_custom_call" | custom-call | tf_op jit(solution)/shard_map/pallas_call | solution.py:597
  71.5 1.2 %finish.1 = (bf16[128,2048]{1,0:T(8,128)(2,1)}, f32[1,128]{1,0:T(1,128)}, bf16[512,768]{1,0:T(8,128)(2,1)}, bf16[384,512]{1,0:T(8,128)(2,1)}) custom-call(bf16[8,32,2048]{2,1,0:T(8,128)(2,1)S(1)} %get-tuple-element.13.rets, bf16[128,256]{1,0:T(8,128)(2,1)S(1)} %get-tuple-element.14.lookup, f32[1,128]{1,0:T(1,128)S(1)} %get-tuple-element.15.ggrad, ...), custom_call_target="tpu_custom_call" | custom-call | tf_op jit(solution)/shard_map/finish/pallas_call | solution.py:660
